TPU v7x, 32 devices: a whole 2x2x4 slice. The times are simulated.
32 devices in a mesh: rep: 2 (over y), span: 2 (over core), seq: 4 (over z), tp: 2 (over x).
Axes of the slice: x: 2, y: 2, z: 4, core: 2. Of those that a mesh axis runs over, the one named last changes fastest.
Arguments:
- queries: bfloat16 [8, 512, 24, 128], P(('rep', 'span'), 'seq', 'tp'), parts along dimension 0, may hold values from -110 to 110
- key_states: bfloat16 [8, 512, 4, 128], P(('rep', 'span'), 'seq', 'tp'), parts along dimension 0, may hold values from -11 to 11
- value_states: bfloat16 [8, 512, 4, 128], P(('rep', 'span'), 'seq', 'tp'), parts along dimension 0, may hold values from -6 to 6
- out_weight: bfloat16 [3072, 6144], P('tp', 'seq'), may hold values from -0.109375 to 0.109375
- noise_table: float32 [64, 6144], P(None, 'tp'), may hold values from 0.5 to 2
- plan: int32 [8], P('rep'), parts along dimension 0, may hold values from 0 to 63
Outputs:
- branch_out: bfloat16 [8, 512, 6144], P(('rep', 'span'), 'seq', 'tp'), parts along dimension 0
There are 2 independent parts, one for each index of `rep`. A program takes and returns all parts, laid end to end along the dimension named above; an argument that names none is the same for every part. Nothing has to cross between parts.
All inputs are finite; a program needn't handle non-finite values.
Results may differ from a plain program's by a relative error of at most 0.014.
Values may be sent and summed in bfloat16 or wider, within the bound.
A program may use at most 128 MiB of HBM per device.

v0:
```python
import jax
import jax.numpy as jnp
from jax import lax
from jax.sharding import PartitionSpec as P


def fold_block(carried, query_rows, key_rows, value_rows, factor):
    maxima, totals, weighted = carried
    scores = (
        jnp.einsum("tkgd,skd->tkgs", query_rows, key_rows, preferred_element_type=jnp.float32)
        * factor
    )
    highest = jnp.maximum(maxima, jnp.max(scores, axis=-1))
    shrink = jnp.exp(maxima - highest)
    weights = jnp.exp(scores - highest[..., None])
    totals = totals * shrink + jnp.sum(weights, axis=-1)
    weighted = weighted * shrink[..., None] + jnp.einsum(
        "tkgs,skd->tkgd",
        weights.astype(jnp.bfloat16),
        value_rows,
        preferred_element_type=jnp.float32,
    )
    return (maxima * 0.0 + highest, totals, weighted)


def per_device(queries, key_states, value_states, out_weight, noise_table, plan):
    ch_dev, tok_dev, heads_local, head_size = queries.shape
    kv_local = key_states.shape[2]
    per_kv = heads_local // kv_local
    span_count = ch_dev * lax.axis_size("span")
    first_span = lax.axis_index("span") * ch_dev
    factor = head_size ** (-0.5)
    grouped = queries.reshape(ch_dev, tok_dev, kv_local, per_kv, head_size)
    start_max = jnp.full((ch_dev, tok_dev, kv_local, per_kv), -1e30, jnp.float32)
    start_tot = jnp.zeros((ch_dev, tok_dev, kv_local, per_kv), jnp.float32)
    start_acc = jnp.zeros((ch_dev, tok_dev, kv_local, per_kv, head_size), jnp.float32)
    span_rows = (
        lax.all_gather(key_states, "seq", axis=1, tiled=True),
        lax.all_gather(value_states, "seq", axis=1, tiled=True),
    )
    key_piece = lax.all_gather(span_rows[0], "span", axis=0, tiled=True)
    value_piece = lax.all_gather(span_rows[1], "span", axis=0, tiled=True)
    new_max = []
    new_tot = []
    new_acc = []
    for q_span in range(ch_dev):
        inner_state = (start_max[q_span], start_tot[q_span], start_acc[q_span])
        for k_span in range(span_count):

            def update(inner, q_span=q_span, k_span=k_span):
                return fold_block(
                    inner, grouped[q_span], key_piece[k_span], value_piece[k_span], factor
                )

            inner_state = lax.cond(
                k_span <= first_span + q_span, update, lambda inner: inner, inner_state
            )
        new_max.append(inner_state[0])
        new_tot.append(inner_state[1])
        new_acc.append(inner_state[2])
    attn = (
        (jnp.stack(new_acc) / jnp.stack(new_tot)[..., None])
        .reshape(ch_dev, tok_dev, heads_local * head_size)
        .astype(jnp.bfloat16)
    )
    columns = jnp.einsum(
        "ctf,fo->cto",
        lax.all_gather(attn, "seq", axis=1, tiled=True),
        out_weight,
        preferred_element_type=jnp.float32,
    )
    partial_out = lax.all_to_all(
        columns.astype(jnp.bfloat16), "seq", split_axis=1, concat_axis=2, tiled=True
    ).astype(columns.dtype)
    summed = lax.psum_scatter(
        partial_out.astype(jnp.bfloat16), "tp", scatter_dimension=2, tiled=True
    ).astype(jnp.float32)
    levels = lax.dynamic_slice_in_dim(plan, first_span, ch_dev)
    picks = (levels[:, None] == jnp.arange(noise_table.shape[0], dtype=jnp.int32)[None, :]).astype(
        jnp.float32
    )
    gates = jnp.dot(picks, noise_table, precision=lax.Precision.HIGHEST)
    return (summed * gates[:, None, :]).astype(jnp.bfloat16)


def solution(mesh):
    placed = (
        P(("rep", "span"), "seq", "tp", None),
        P(("rep", "span"), "seq", "tp", None),
        P(("rep", "span"), "seq", "tp", None),
        P("tp", "seq"),
        P(None, "tp"),
        P("rep"),
    )
    return jax.shard_map(
        per_device,
        mesh=mesh,
        in_specs=placed,
        out_specs=P(("rep", "span"), "seq", "tp"),
        check_vma=False,
    )
```

profile of v0, /device:TPU:0, one launch (start us, length us, event | category | flops | bytes accessed | tf_op | source)
XLA Modules:
  0.0 320.5 jit_solution(18199733619609409647)
XLA Ops:
  6.5 1.0 copy.63
  7.5 18.0 %all_gather.15 = bf16[2,512,2,128]{3,1,2,0:T(8,128)(2,1)} all-gather(bf16[2,128,2,128]{3,1,2,0:T(8,128)(2,1)S(1)} %copy.63), channel_id=1, replica_groups=mesh['rep'=2,'span'=2,'seq'=4,'tp'=2] {'seq'}, dimensions={1}, use_global_device_ids=true | all-gather | bytes 655360 | tf_op jit(solution)/shard_map/all_gather | solution.py:38
  25.6 0.9 copy.64
  26.5 17.0 %all_gather.17 = bf16[2,512,2,128]{3,1,2,0:T(8,128)(2,1)} all-gather(bf16[2,128,2,128]{3,1,2,0:T(8,128)(2,1)S(1)} %copy.64), channel_id=1, replica_groups=mesh['rep'=2,'span'=2,'seq'=4,'tp'=2] {'seq'}, dimensions={1}, use_global_device_ids=true | all-gather | bytes 655360 | tf_op jit(solution)/shard_map/all_gather | solution.py:39
  43.7 9.6 %all-gather.6.cloned.1.call-done = bf16[4,512,2,128]{3,1,2,0:T(8,128)(2,1)} async-done(((bf16[2,512,2,128]{3,1,2,0:T(8,128)(2,1)}), bf16[4,512,2,128]{3,1,2,0:T(8,128)(2,1)}) %all-gather.6.cloned.1.call-update) | async-done | bytes 1048592 | tf_op jit(solution)/shard_map/all_gather | solution.py:42
  53.3 6.1 %conditional.12 = (f32[128,2,6]{0,2,1:T(8,128)}, f32[128,2,6]{0,2,1:T(8,128)S(1)}, f32[128,2,6,128]{3,0,2,1:T(8,128)S(1)}) conditional(s32[]{:T(128)} %convert_element_type.70, () %tuple.93, (bf16[4,512,2,128]{3,1,2,0:T(8,128)(2,1)}, bf16[2,128,2,6,128]{4,1,3,2,0:T(8,128)(2,1)}, bf16[4,512,2,128]{3,1,2,0:T(8,128)(2,1)}) %tuple.190), branch_computations={%region_16.0_spmd, %region_17.0_spmd} | conditional | flops 409147392 | bytes 11210776 | solution.py:55
  53.3 1.7 bitcast_reduce_fusion.4
  55.6 1.2 fusion.85
  57.5 1.9 fusion.93
  59.4 6.2 %conditional.13 = ((f32[128,2,6]{0,2,1:T(8,128)}, f32[128,2,6]{0,2,1:T(8,128)S(1)}, f32[128,2,6,128]{3,0,2,1:T(8,128)S(1)})) conditional(s32[]{:T(128)} %convert_element_type.69, (f32[128,2,6]{0,2,1:T(8,128)}, f32[128,2,6]{0,2,1:T(8,128)S(1)}, f32[128,2,6,128]{3,0,2,1:T(8,128)S(1)}) %conditional.12, (f32[128,2,6]{0,2,1:T(8,128)}, ...), branch_computations={%region_20.0_spmd, %region_21.0_spmd} | conditional | flops 409344000 | bytes 12032032 | solution.py:55
  59.4 1.7 bitcast_reduce_fusion.5
  62.3 0.7 multiply_add_fusion.4
  63.6 2.0 fusion.115
  65.6 6.1 %conditional.8 = (f32[128,2,6]{0,2,1:T(8,128)}, f32[128,2,6]{0,2,1:T(8,128)S(1)}, f32[128,2,6,128]{3,0,2,1:T(8,128)S(1)}) conditional(s32[]{:T(128)} %convert_element_type.66, () %tuple.87, (bf16[4,512,2,128]{3,1,2,0:T(8,128)(2,1)}, bf16[2,128,2,6,128]{4,1,3,2,0:T(8,128)(2,1)}, bf16[4,512,2,128]{3,1,2,0:T(8,128)(2,1)}) %tuple.193), branch_computations={%region_0.0_spmd, %region_1.0_spmd} | conditional | flops 409147392 | bytes 11210776 | solution.py:55
  65.6 1.7 bitcast_reduce_fusion
  67.9 1.2 fusion.2
  69.1 0.7 fusion.21
  69.8 1.9 fusion.10
  72.0 1.5 conditional.15
  72.2 1.2 copy.102
  73.4 1.4 conditional.11
  73.7 1.2 copy.100
  75.0 1.6 copy.73
  76.6 2.9 fusion.171
  79.6 93.0 %all-gather.8.cloned.1.call-done = bf16[2,512,1536]{2,1,0:T(8,128)(2,1)} async-done(((bf16[2,128,1536]{2,1,0:T(8,128)(2,1)}), bf16[2,512,1536]{2,1,0:T(8,128)(2,1)}) %all-gather.8.cloned.1.call-update) | async-done | bytes 3145744 | tf_op jit(solution)/shard_map/all_gather | solution.py:68
  172.6 8.1 %fusion.168 = bf16[2,512,1536]{2,1,0:T(8,128)(2,1)S(1)} fusion(bf16[2,512,1536]{2,1,0:T(8,128)(2,1)} %all-gather.8.cloned.1.call-done, bf16[1536,1536]{1,0:T(8,128)(2,1)} %param.25), kind=kOutput, calls=%fused_computation.166 | convolution fusion | flops 4833411072 | bytes 11010048 | tf_op jit(solution)/shard_map/ctf,fo->cto/dot_general | solution.py:66
  180.7 3.2 %copy.74 = bf16[2,512,1536]{2,0,1:T(2,128)(2,1)S(1)} copy(bf16[2,512,1536]{2,1,0:T(8,128)(2,1)S(1)} %fusion.168) | data formatting | bytes 6291456 | tf_op jit(solution)/shard_map/convert_element_type | solution.py:73
  183.9 73.3 %all_to_all.18 = bf16[2,512,1536]{2,0,1:T(2,128)(2,1)S(1)} all-to-all(bf16[2,512,1536]{2,0,1:T(2,128)(2,1)S(1)} %copy.74), channel_id=1, replica_groups=mesh['rep'=2,'span'=2,'seq'=4,'tp'=2] {'seq'}, dimensions={1} | all-to-all | bytes 6291456 | tf_op jit(solution)/shard_map/all_to_all | solution.py:72
  257.2 4.1 %copy.75 = bf16[2,128,4,1536]{3,2,1,0:T(4,128)(2,1)} copy(bf16[2,128,4,1536]{3,0,1,2:T(2,128)(2,1)S(1)} %bitcast.326) | data formatting | bytes 6291456 | tf_op jit(solution)/shard_map/all_to_all | solution.py:72
  261.3 6.9 %all_to_all.16 = bf16[2,128,6144]{2,1,0:T(8,128)(2,1)} reshape(bf16[2,128,4,1536]{3,2,1,0:T(4,128)(2,1)} %copy.75) | data formatting | bytes 6291456 | tf_op jit(solution)/shard_map/all_to_all | solution.py:72
  269.4 41.7 %reduce-scatter.2.cloned.1.call-done = bf16[2,128,3072]{2,1,0:T(8,128)(2,1)} async-done(((bf16[2,128,6144]{2,1,0:T(8,128)(2,1)}), bf16[2,128,3072]{2,1,0:T(8,128)(2,1)}) %reduce-scatter.2.cloned.1.call-update) | async-done | bytes 1572880 | tf_op jit(solution)/shard_map/reduce_scatter | solution.py:75
  311.1 2.9 multiply_convert_fusion
  (28 shorter events, 5.9 us)
Async XLA Ops:
  6.5 262.4 %copy-start = (f32[64,3072]{1,0:T(8,128)S(1)}, f32[64,3072]{1,0:T(8,128)}, u32[]{:S(2)}) copy-start(f32[64,3072]{1,0:T(8,128)} %param.26) | copy-start | bytes 2359300
  6.5 37.2 %all-gather.4.cloned.1.call-start = ((), (), s32[]{:S(2)}) async-start(), calls=%async_computation.2 | async-start | bytes 1572864 | tf_op jit(solution)/shard_map/all_gather | solution.py:41
  25.6 27.7 %all-gather.6.cloned.1.call-start = ((), (), s32[]{:S(2)}) async-start(), calls=%async_computation.3 | async-start | bytes 1572864 | tf_op jit(solution)/shard_map/all_gather | solution.py:42
  43.6 129.0 %all-gather.8.cloned.1.call-start = ((), (), s32[]{:S(2)}) async-start(), calls=%async_computation.4 | async-start | bytes 3932160 | tf_op jit(solution)/shard_map/all_gather | solution.py:68
  79.6 231.5 %reduce-scatter.2.cloned.1.call-start = ((), (), s32[]{:S(2)}) async-start(), calls=%async_computation.5 | async-start | bytes 4718592 | tf_op jit(solution)/shard_map/reduce_scatter | solution.py:75
  268.3 0.7 copy-start.5
Sparse Core Ops, SparseCore 0:
  25.7 10.8 all-gather.3
  43.7 9.5 all-gather.5
  79.7 92.8 all-gather.7
  268.4 42.6 reduce-scatter.1
where the time goes:
time: 322 us; the launch traced here: 321 us
  waiting for transfers between devices  144 us (45%)
  blocking collectives  108 us (34%)
  local copies, waits for them, and re-layouts  22.1 us (7%)
  matrix products  19.2 us (6%)
  between operations  13.2 us (4%)
  other arithmetic  12.9 us (4%)
    all_gather x1, waiting for transfers between devices, per_device(): lax.all_gather(attn, 'seq', axis=1, tiled=True)  93 us
    all_to_all x1, blocking collectives, per_device(): lax.all_to_all(columns.astype(jnp.bfloat16), 'seq', split_axis=1, concat_...  73.3 us
    reduce_scatter x1, waiting for transfers between devices, per_device(): lax.psum_scatter(partial_out.astype(jnp.bfloat16), 'tp', scatter_dimensio...  41.7 us
    all_gather x1, blocking collectives, per_device(): lax.all_gather(key_states, 'seq', axis=1, tiled=True)  18 us
    all_gather x1, blocking collectives, per_device(): lax.all_gather(value_states, 'seq', axis=1, tiled=True)  17 us
    all_to_all x2, local copies, waits for them, and re-layouts, per_device(): lax.all_to_all(columns.astype(jnp.bfloat16), 'seq', split_axis=1, concat_...  11 us
    all_gather x1, waiting for transfers between devices, per_device(): value_piece = lax.all_gather(span_rows[1], 'span', axis=0, tiled=True)  9.6 us
    dot_general x1, matrix products, per_device(): jnp.einsum('ctf,fo->cto', lax.all_gather(attn, 'seq', axis=1, tiled=True)...  8.06 us
  transfers between devices with their start and end apart: 4, of which 3 were waited for; matrix products, arithmetic and copies ran while one was open for 0% of the time, Pallas kernels for 0%

commit v1 on v0

--- a/solution.py
+++ b/solution.py
@@ -1,7 +1,310 @@
+import functools
+import math
+
 import jax
 import jax.numpy as jnp
 from jax import lax
+from jax.experimental import pallas as pl
+from jax.experimental.pallas import tpu as pltpu
 from jax.sharding import PartitionSpec as P
+
+MESH = pl.DeviceIdType.MESH
+
+
+def fused_kernel(
+    parts, plan_ref, q_ref, kv_ref, noise_ref, w_ref, out_ref,
+    kvbuf, wbuf, abuf, pbuf, xsend, xbuf,
+    kv_send, kv_recv, kvc, loc, wz_send, wc_send, wy_send,
+    wz_recv, wc_recv, wy_recv, x_send, x_recv,
+):
+    y, c = lax.axis_index("rep"), lax.axis_index("span")
+    z, t = lax.axis_index("seq"), lax.axis_index("tp")
+    n = lax.axis_size("seq")
+    cores, tps = lax.axis_size("span"), lax.axis_size("tp")
+    spans, heads, tok, hd = q_ref.shape
+    kvh = kv_ref.shape[1]
+    per_kv = heads // kvh
+    depth, cols = w_ref.shape
+    quarter = depth // (cores * lax.axis_size("rep"))
+    sub = cols // parts
+    owned = n // tps
+    first = c * spans
+    steps = (n - 1) * parts
+    scale = hd ** (-0.5) * math.log2(math.e)
+
+    def rows(yy, cc):
+        return pl.ds(pl.multiple_of((yy * cores + cc) * quarter, quarter), quarter)
+
+    def remote(src, dst, send, recv, where):
+        return pltpu.make_async_remote_copy(
+            src_ref=src, dst_ref=dst, send_sem=send, recv_sem=recv,
+            device_id=where, device_id_type=MESH,
+        )
+
+    def z_copy(s, j, way, own):
+        dst = wbuf.at[s, j, rows(y, c)]
+        src = w_ref.at[rows(y, c), pl.ds(pl.multiple_of(j * sub, sub), sub)] if own else dst
+        to = z - 1 if way == 0 else z + 1
+        return remote(src, dst, wz_send.at[way, s, j], wz_recv.at[s, j], {"seq": to})
+
+    def core_copy(s, j, kind):
+        part = wbuf.at[s, j, rows(y if kind == 0 else 1 - y, c)]
+        return remote(part, part, wc_send.at[kind, s, j], wc_recv.at[kind, s, j], {"span": 1 - c})
+
+    def y_copy(s, j):
+        part = wbuf.at[s, j, rows(y, c)]
+        return remote(part, part, wy_send.at[s, j], wy_recv.at[s, j], {"rep": 1 - y})
+
+    def x_copy(s, j):
+        at = lax.rem(s, owned)
+        return remote(xsend.at[at, j], xbuf.at[at, j], x_send.at[at, j], x_recv.at[at, j], {"tp": 1 - t})
+
+    def kv_copy(to, at):
+        return remote(
+            kv_ref, kvbuf.at[pl.ds(first, spans), :, :, z], kv_send.at[to], kv_recv.at[at], {"seq": to}
+        )
+
+    def kv_core():
+        part = kvbuf.at[pl.ds(0, spans)]
+        return remote(part, part, kvc.at[0], kvc.at[1], {"span": 1 - c})
+
+    def local_w(j):
+        return pltpu.make_async_copy(
+            w_ref.at[:, pl.ds(pl.multiple_of(j * sub, sub), sub)], wbuf.at[z, j], loc.at[j]
+        )
+
+    def local_kv():
+        return pltpu.make_async_copy(
+            kv_ref, kvbuf.at[pl.ds(first, spans), :, :, z], loc.at[parts]
+        )
+
+    barrier = pltpu.get_barrier_semaphore()
+    for peer in range(n):
+        @pl.when(z != peer)
+        def _(peer=peer):
+            pl.semaphore_signal(barrier, inc=1, device_id={"seq": peer}, device_id_type=MESH)
+    pl.semaphore_signal(barrier, inc=1, device_id={"rep": 1 - y}, device_id_type=MESH)
+    pl.semaphore_signal(barrier, inc=1, device_id={"span": 1 - c}, device_id_type=MESH)
+    pl.semaphore_signal(barrier, inc=1, device_id={"tp": 1 - t}, device_id_type=MESH)
+    pl.semaphore_wait(barrier, n - 1 + 3)
+
+    local_kv().start()
+    for peer in range(n):
+        @pl.when(z != peer)
+        def _(peer=peer):
+            kv_copy(peer, z).start()
+    for j in range(parts):
+        @pl.when(z > 0)
+        def _(j=j):
+            z_copy(z, j, 0, True).start()
+
+        @pl.when(z < n - 1)
+        def _(j=j):
+            z_copy(z, j, 1, True).start()
+    for j in range(parts):
+        local_w(j).start()
+
+    local_kv().wait()
+    for peer in range(n):
+        @pl.when(z != peer)
+        def _(peer=peer):
+            kv_copy(peer, peer).wait_recv()
+
+    @pl.when(c == 0)
+    def _():
+        kv_core().start()
+
+    @pl.when(c != 0)
+    def _():
+        kv_core().wait_recv()
+
+    def each(e, low, do):
+        ok = jnp.logical_and(e >= low, e < steps)
+        d, j = e // parts + 1, e % parts
+        for sign in (-1, 1):
+            s = z + sign * d
+
+            @pl.when(jnp.logical_and(ok, jnp.logical_and(s >= 0, s < n)))
+            def _(s=s, sign=sign):
+                do(s, j, sign)
+
+    def arrive(s, j, sign):
+        way = 0 if sign > 0 else 1
+        z_copy(s, j, way, False).wait_recv()
+
+        @pl.when((z > 0) if way == 0 else (z < n - 1))
+        def _():
+            z_copy(s, j, way, False).start()
+
+        y_copy(s, j).start()
+        core_copy(s, j, 0).start()
+
+    def pass_on(s, j, sign):
+        y_copy(s, j).wait_recv()
+        core_copy(s, j, 1).start()
+
+    def project(s, j):
+        part = jnp.dot(abuf[...], wbuf[s, j], preferred_element_type=jnp.float32)
+        at = lax.rem(s, owned)
+
+        @pl.when(s // owned == t)
+        def _():
+            pbuf[at, j] = part
+
+        @pl.when(s // owned != t)
+        def _():
+            xsend[at, j] = part.astype(jnp.bfloat16)
+            x_copy(s, j).start()
+
+    def gather_project(s, j, sign):
+        core_copy(s, j, 0).wait_recv()
+        core_copy(s, j, 1).wait_recv()
+        project(s, j)
+
+    def finish(s, j, sign):
+        @pl.when(s // owned == t)
+        def _():
+            x_copy(s, j).wait_recv()
+            at = lax.rem(s, owned)
+            where = pl.ds(pl.multiple_of(at * cols + j * sub, 128), sub)
+            for i in range(spans):
+                level = plan_ref[first + i]
+                gate = noise_ref[pl.ds(level, 1), where]
+                mine = pl.ds(i * tok, tok)
+                total = pbuf[at, j, mine, :] + xbuf[at, j, mine, :].astype(jnp.float32)
+                out_ref[mine, where] = (total * gate).astype(out_ref.dtype)
+
+    units = spans * kvh
+    lead = per_kv * tok
+
+    def attend(u, carry):
+        i, g = u // kvh, u % kvh
+        query = q_ref[i, pl.ds(g * per_kv, per_kv)].reshape(lead, hd)
+
+        def fold(k, state):
+            top, total, mixed = state
+            keys = kvbuf[k, g, 0].reshape(n * tok, hd)
+            values = kvbuf[k, g, 1].reshape(n * tok, hd)
+            scores = lax.dot_general(
+                query, keys, (((1,), (1,)), ((), ())), preferred_element_type=jnp.float32
+            )
+            high = jnp.maximum(top, jnp.max(scores, axis=1, keepdims=True))
+            shrink = jnp.exp2((top - high) * scale)
+            weights = jnp.exp2((scores - high) * scale)
+            total = total * shrink + jnp.sum(weights, axis=1, keepdims=True)
+            mixed = mixed * shrink + jnp.dot(
+                weights.astype(jnp.bfloat16), values, preferred_element_type=jnp.float32
+            )
+            return high, total, mixed
+
+        start = (
+            jnp.full((lead, 1), -1e30, jnp.float32),
+            jnp.zeros((lead, 1), jnp.float32),
+            jnp.zeros((lead, hd), jnp.float32),
+        )
+        _, total, mixed = lax.fori_loop(0, first + i + 1, fold, start)
+        result = (mixed / total).astype(jnp.bfloat16).reshape(per_kv, tok, hd)
+        for h in range(per_kv):
+            abuf[
+                pl.ds(pl.multiple_of(i * tok, tok), tok),
+                pl.ds(pl.multiple_of((g * per_kv + h) * hd, hd), hd),
+            ] = result[h]
+        each(u, 0, arrive)
+        each(u - 1, 0, pass_on)
+        return carry
+
+    lax.fori_loop(0, units, attend, 0)
+
+    def own(j, carry):
+        local_w(j).wait()
+        project(z, j)
+        return carry
+
+    lax.fori_loop(0, parts, own, 0)
+
+    def run(e, carry):
+        each(e, units, arrive)
+        each(e - 1, units - 1, pass_on)
+        each(e - 2, 0, gather_project)
+        each(e - 3, 0, finish)
+        return carry
+
+    lax.fori_loop(2, units, lambda e, carry: (each(e - 2, 0, gather_project), carry)[1], 0)
+    lax.fori_loop(0, parts, lambda j, carry: (finish(z, j, 0), carry)[1], 0)
+    lax.fori_loop(3, units, lambda e, carry: (each(e - 3, 0, finish), carry)[1], 0)
+    lax.fori_loop(units, max(steps, units) + 3, run, 0)
+
+    for peer in range(n):
+        @pl.when(z != peer)
+        def _(peer=peer):
+            kv_copy(peer, z).wait_send()
+
+    @pl.when(c == 0)
+    def _():
+        kv_core().wait_send()
+
+    def drain(f, carry):
+        s, j = f // parts, f % parts
+
+        @pl.when(jnp.logical_and(z > 0, s >= z))
+        def _():
+            z_copy(s, j, 0, False).wait_send()
+
+        @pl.when(jnp.logical_and(z < n - 1, s <= z))
+        def _():
+            z_copy(s, j, 1, False).wait_send()
+
+        @pl.when(s != z)
+        def _():
+            core_copy(s, j, 0).wait_send()
+            core_copy(s, j, 1).wait_send()
+            y_copy(s, j).wait_send()
+
+        @pl.when(s // owned != t)
+        def _():
+            x_copy(s, j).wait_send()
+
+        return carry
+
+    lax.fori_loop(0, n * parts, drain, 0)
+
+
+def fused(parts, queries, key_states, value_states, out_weight, noise_table, plan):
+    spans, tok, heads, hd = queries.shape
+    kvh = key_states.shape[2]
+    depth, cols = out_weight.shape
+    n, tps, cores = lax.axis_size("seq"), lax.axis_size("tp"), lax.axis_size("span")
+    sub, owned, wide = cols // parts, n // tps, noise_table.shape[1]
+    q = jnp.transpose(queries, (0, 2, 1, 3))
+    kv = jnp.stack([key_states, value_states], axis=0).transpose(1, 3, 0, 2, 4)
+    vmem = pl.BlockSpec(memory_space=pltpu.VMEM)
+    dma = pltpu.SemaphoreType.DMA
+    out = pl.pallas_call(
+        functools.partial(fused_kernel, parts),
+        out_shape=jax.ShapeDtypeStruct((spans * tok, wide), jnp.bfloat16),
+        in_specs=[
+            pl.BlockSpec(memory_space=pltpu.SMEM), vmem, vmem, vmem,
+            pl.BlockSpec(memory_space=pl.ANY),
+        ],
+        out_specs=vmem,
+        scratch_shapes=[
+            pltpu.VMEM((spans * cores, kvh, 2, n, tok, hd), jnp.bfloat16),
+            pltpu.VMEM((n, parts, depth, sub), jnp.bfloat16),
+            pltpu.VMEM((spans * tok, depth), jnp.bfloat16),
+            pltpu.VMEM((owned, parts, spans * tok, sub), jnp.float32),
+            pltpu.VMEM((owned, parts, spans * tok, sub), jnp.bfloat16),
+            pltpu.VMEM((owned, parts, spans * tok, sub), jnp.bfloat16),
+            dma((n,)), dma((n,)), dma((2,)), dma((parts + 1,)),
+            dma((2, n, parts)), dma((2, n, parts)), dma((n, parts)),
+            dma((n, parts)), dma((2, n, parts)), dma((n, parts)),
+            dma((owned, parts)), dma((owned, parts)),
+        ],
+        compiler_params=pltpu.CompilerParams(
+            collective_id=0, has_side_effects=True, vmem_limit_bytes=60 * 1024 * 1024
+        ),
+        name="relay_attention",
+    )(plan, q, kv, noise_table, out_weight)
+    return out.reshape(spans, tok, wide)
 
 
 def fold_block(carried, query_rows, key_rows, value_rows, factor):
@@ -83,6 +386,24 @@
     return (summed * gates[:, None, :]).astype(jnp.bfloat16)
 
 
+def choose_parts(cols):
+    for parts in (4, 3, 2, 1):
+        if cols % (parts * 128) == 0:
+            return parts
+    return 0
+
+
+def dispatch(queries, key_states, value_states, out_weight, noise_table, plan):
+    depth, cols = out_weight.shape
+    copies = lax.axis_size("rep") * lax.axis_size("span")
+    parts = choose_parts(cols)
+    pairs = all(lax.axis_size(name) == 2 for name in ("rep", "span", "tp"))
+    args = (queries, key_states, value_states, out_weight, noise_table, plan)
+    if pairs and parts and depth % (copies * 16) == 0 and lax.axis_size("seq") % 2 == 0:
+        return fused(parts, *args)
+    return per_device(*args)
+
+
 def solution(mesh):
     placed = (
         P(("rep", "span"), "seq", "tp", None),
@@ -93,7 +414,7 @@
         P("rep"),
     )
     return jax.shard_map(
-        per_device,
+        dispatch,
         mesh=mesh,
         in_specs=placed,
         out_specs=P(("rep", "span"), "seq", "tp"),

time: 322 us -> 147 us (0.46)
  waiting for transfers between devices: 144 us -> 0 us
  Pallas kernels: 0 us -> 140 us
  blocking collectives: 108 us -> 0 us
  matrix products: 19.2 us -> 0 us
  local copies, waits for them, and re-layouts: 22.1 us -> 3.65 us
  between operations: 13.2 us -> 0.01 us
  other arithmetic: 12.9 us -> 0.73 us
    pallas_call x0 -> x1, Pallas kernels: none -> 140 us  [fused(): pl.pallas_call(functools.partial(fused_kernel, parts), out_shape=jax.Shap...]
    all_gather x3 -> x0, waiting for transfers between devices: 103 us -> none  [the longest x1 93 us: per_device(): lax.all_gather(attn, 'seq', axis=1, tiled=True)]
    all_to_all x1 -> x0, blocking collectives: 73.3 us -> none  [per_device(): lax.all_to_all(columns.astype(jnp.bfloat16), 'seq', split_axis=1, concat_...]
    reduce_scatter x1 -> x0, waiting for transfers between devices: 41.7 us -> none  [per_device(): lax.psum_scatter(partial_out.astype(jnp.bfloat16), 'tp', scatter_dimensio...]
    all_gather x2 -> x0, blocking collectives: 35 us -> none  [the longest x1 18 us: per_device(): lax.all_gather(key_states, 'seq', axis=1, tiled=True)]
    dot_general x8 -> x0, matrix products: 19.2 us -> none  [the longest x1 8.06 us: per_device(): jnp.einsum('ctf,fo->cto', lax.all_gather(attn, 'seq', axis=1, tiled=True)...]
    all_to_all x2 -> x0, local copies, waits for them, and re-layouts: 11 us -> none  [per_device(): lax.all_to_all(columns.astype(jnp.bfloat16), 'seq', split_axis=1, concat_...]
    convert_element_type x2 -> x0, other arithmetic: 5.85 us -> none  [the longest x1 2.95 us: per_device(): attn = (jnp.stack(new_acc) / jnp.stack(new_tot)[..., None]).reshape(ch_de...]
  transfers between devices with their start and end apart: 4 -> 0, of which waited for: 3 -> 0; matrix products, arithmetic and copies ran while one was open for 0% -> 0% of each run, Pallas kernels for 0% -> 0%
where the time goes in v1:
time: 147 us; the launch traced here: 145 us
  Pallas kernels  140 us (95%)
  local copies, waits for them, and re-layouts  3.65 us (2%)
    pallas_call x1, Pallas kernels, fused(): pl.pallas_call(functools.partial(fused_kernel, parts), out_shape=jax.Shap...  140 us

profile of v1, /device:TPU:0, one launch (start us, length us, event | category | flops | bytes accessed | tf_op | source)
XLA Modules:
  0.0 144.8 jit_solution(10577507041221899716)
XLA Ops:
  0.0 1.0 copy_bitcast_fusion
  1.0 0.7 maximum_bitcast_fusion.kv_ref
  1.7 140.4 %relay_attention.1 = bf16[256,3072]{1,0:T(8,128)(2,1)} custom-call(s32[4]{0:T(128)} %plan_ref.1, bf16[2,12,128,128]{3,2,1,0:T(8,128)(2,1)} %bitcast.9, bf16[2,2,2,128,128]{4,3,2,1,0:T(8,128)(2,1)} %maximum_bitcast_fusion.kv_ref, f32[64,3072]{1,0:T(8,128)} %noise_ref.1, bf16[1536,1536]{1,0:T(8,128)(2,1)} %w_ref.1), custom_call_target="tpu_custom_call" | custom-call | tf_op jit(solution)/shard_map/relay_attention/pallas_call | solution.py:282
  142.2 2.7 %copy.12 = bf16[2,128,3072]{2,1,0:T(8,128)(2,1)} copy(bf16[2,128,3072]{2,1,0:T(8,128)(2,1)} %bitcast.8) | data formatting | bytes 3145728

commit v2 on v1

--- a/solution.py
+++ b/solution.py
@@ -175,6 +175,7 @@
                 out_ref[mine, where] = (total * gate).astype(out_ref.dtype)
 
     units = spans * kvh
+    lag = units - 1
     lead = per_kv * tok
 
     def attend(u, carry):
@@ -210,7 +211,7 @@
                 pl.ds(pl.multiple_of((g * per_kv + h) * hd, hd), hd),
             ] = result[h]
         each(u, 0, arrive)
-        each(u - 1, 0, pass_on)
+        each(u - lag, 0, pass_on)
         return carry
 
     lax.fori_loop(0, units, attend, 0)
@@ -224,15 +225,13 @@
 
     def run(e, carry):
         each(e, units, arrive)
-        each(e - 1, units - 1, pass_on)
-        each(e - 2, 0, gather_project)
-        each(e - 3, 0, finish)
+        each(e - lag, units - lag, pass_on)
+        each(e - lag - 1, 0, gather_project)
+        each(e - lag - 3, 0, finish)
         return carry
 
-    lax.fori_loop(2, units, lambda e, carry: (each(e - 2, 0, gather_project), carry)[1], 0)
     lax.fori_loop(0, parts, lambda j, carry: (finish(z, j, 0), carry)[1], 0)
-    lax.fori_loop(3, units, lambda e, carry: (each(e - 3, 0, finish), carry)[1], 0)
-    lax.fori_loop(units, max(steps, units) + 3, run, 0)
+    lax.fori_loop(units, max(steps, units) + lag + 3, run, 0)
 
     for peer in range(n):
         @pl.when(z != peer)
@@ -387,7 +386,7 @@
 
 
 def choose_parts(cols):
-    for parts in (4, 3, 2, 1):
+    for parts in (6, 3, 2, 1):
         if cols % (parts * 128) == 0:
             return parts
     return 0

time: 147 us -> 137 us (0.932)
  Pallas kernels: 140 us -> 131 us
    pallas_call x1, Pallas kernels: 140 us -> 131 us  [fused(): pl.pallas_call(functools.partial(fused_kernel, parts), out_shape=jax.Shap...]
where the time goes in v2:
time: 137 us; the launch traced here: 136 us
  Pallas kernels  131 us (96%)
  local copies, waits for them, and re-layouts  3.65 us (3%)
    pallas_call x1, Pallas kernels, fused(): pl.pallas_call(functools.partial(fused_kernel, parts), out_shape=jax.Shap...  131 us

profile of v2, /device:TPU:0, one launch (start us, length us, event | category | flops | bytes accessed | tf_op | source)
XLA Modules:
  0.0 135.9 jit_solution(5738295177670229224)
XLA Ops:
  0.0 1.0 copy_bitcast_fusion
  1.0 0.7 maximum_bitcast_fusion.kv_ref
  1.7 131.5 %relay_attention.1 = bf16[256,3072]{1,0:T(8,128)(2,1)} custom-call(s32[4]{0:T(128)} %plan_ref.1, bf16[2,12,128,128]{3,2,1,0:T(8,128)(2,1)} %bitcast.9, bf16[2,2,2,128,128]{4,3,2,1,0:T(8,128)(2,1)} %maximum_bitcast_fusion.kv_ref, f32[64,3072]{1,0:T(8,128)} %noise_ref.1, bf16[1536,1536]{1,0:T(8,128)(2,1)} %w_ref.1), custom_call_target="tpu_custom_call" | custom-call | tf_op jit(solution)/shard_map/relay_attention/pallas_call | solution.py:281
  133.2 2.7 %copy.12 = bf16[2,128,3072]{2,1,0:T(8,128)(2,1)} copy(bf16[2,128,3072]{2,1,0:T(8,128)(2,1)} %bitcast.8) | data formatting | bytes 3145728
